TPU v7x, 256 devices: a whole 4x4x8 slice. The times are simulated.
256 devices in a mesh: blk: 128 (over z_lo, y, x, core), rep: 2 (over z_hi).
Axes of the slice: x: 4, y: 4, z: 8 (z_hi: 2, z_lo: 4; z = z_hi * 4 + z_lo), core: 2. Of those that a mesh axis runs over, the one named last changes fastest.
Arguments:
- load_coef: bfloat16 [256, 2049, 256], P('blk', None, 'rep'), parts along dimension 2, may hold values from -0.29882812 to 0.29882812
- legendre: bfloat16 [256, 2049, 1024], P('blk'), may hold values from -0.125 to 0.125
- slab_orders: int32 [256], replicated, may hold values from 0 to 1023, as said below
- cycle_rows: int32 [1024], replicated, may hold values from 0 to 1023, each once
Outputs:
- potential: bfloat16 [1024, 128, 4096], P('blk', 'rep'), parts along dimension 1
- energy: float32 [128], P('rep'), parts along dimension 0
There are 2 independent parts, one for each index of `rep`. A program takes and returns all parts, laid end to end along the dimension named above; an argument that names none is the same for every part. Nothing has to cross between parts.
Inputs may be any that keep to these rules, and one draw needn't show every extreme that they name: `slab_orders`: values are distinct and below (2048) / 2. `cycle_rows`: each cycle appears once.
All inputs are finite; a program needn't handle non-finite values.
Results may differ from a plain program's by a relative error of at most 0.0055.
Values may be sent and summed in bfloat16 or wider, within the bound.
A program may use at most 128 MiB of HBM per device.

v0:
```python
import functools
import math

import jax
import jax.numpy as jnp
from jax import lax
from jax.experimental import pallas as pl
from jax.experimental.pallas import tpu as pltpu
from jax.sharding import PartitionSpec as P

NLON = 4096
LANES = 128
MESH = pl.DeviceIdType.MESH


def spectra_kernel(pairs, orders_ref, table_ref, coef_ref, rows_ref, send_ref, energy_ref, masked, spectra, sorted_rows, staging):
    step = pl.program_id(0)
    first_pair = lax.axis_index("blk") * pairs
    slab_rows, _, block = table_ref.shape
    packed_rows = slab_rows * pairs
    streams = masked.shape[0] // (2 * pairs)

    @pl.when(step == 0)
    def _():
        packed = coef_ref[...].reshape(packed_rows, streams)
        flipped = jnp.transpose(jnp.concatenate([packed, jnp.zeros((masked.shape[1] - packed_rows, streams), packed.dtype)], axis=0).astype(jnp.float32))
        packed_id = lax.broadcasted_iota(jnp.int32, flipped.shape, 1)
        row_id = packed_id // pairs
        pair_id = packed_id % pairs
        for pair in range(pairs):
            lower = row_id < slab_rows - 1 - orders_ref[first_pair + pair]
            mine = pair_id == pair
            for half in range(2):
                keep = mine & (lower if half == 0 else ~lower)
                start = (2 * pair + half) * streams
                masked[start : start + streams, :] = jnp.where(keep, flipped, 0.0).astype(jnp.bfloat16)

    product = jnp.dot(masked[:, :packed_rows], table_ref[...].reshape(packed_rows, block), preferred_element_type=jnp.float32)
    spectra[:, pl.ds(pl.multiple_of(step * block, block), block)] = product.astype(jnp.bfloat16)

    @pl.when(step == pl.num_programs(0) - 1)
    def _():
        lat_count = spectra.shape[1]
        fields = streams // 2
        kinds = 4 * pairs
        columns = jnp.transpose(rows_ref[...].astype(jnp.float32))
        cycle_id = lax.broadcasted_iota(jnp.int32, (LANES, lat_count), 1).astype(jnp.float32)
        total = jnp.zeros((1, kinds * fields), jnp.float32)
        half = LANES // 2
        batch = min(4, lat_count // LANES)
        for first_part in range(0, lat_count // LANES, batch):
            chosen = jnp.concatenate(
                [(columns[:, first_part + i : first_part + i + 1] == cycle_id).astype(jnp.float32).astype(jnp.bfloat16) for i in range(batch)],
                axis=0,
            )
            rows = lax.dot_general(chosen, spectra[...], (((1,), (1,)), ((), ())), preferred_element_type=jnp.float32)
            total = total + jnp.sum(rows * rows, axis=0, keepdims=True)
            for part in range(first_part, first_part + batch):
                offset = (part - first_part) * LANES
                for order in range(2 * pairs):
                    sorted_rows[part, order] = rows[offset : offset + LANES, order * streams : (order + 1) * streams]
                    even = sorted_rows[part, order, pl.ds(0, half, stride=2), :]
                    odd = sorted_rows[part, order, pl.ds(1, half, stride=2), :]
                    real = jnp.concatenate([even[:, :fields], odd[:, :fields]], axis=1)
                    imag = jnp.concatenate([even[:, fields:], odd[:, fields:]], axis=1)
                    first = part * half * kinds + 2 * order
                    staging[pl.ds(first, half, stride=kinds), :] = real
                    staging[pl.ds(first + 1, half, stride=kinds), :] = imag
        energy = jnp.zeros((1, streams), jnp.float32)
        lane_id = lax.broadcasted_iota(jnp.int32, (1, streams), 1)
        for index in range(2 * pairs):
            part = total[:, index * streams : (index + 1) * streams]
            if index % 2 == 0:
                constant = orders_ref[first_pair + index // 2] == 0
                weight = jnp.where(constant, jnp.where(lane_id < fields, 1.0, 0.0), 2.0)
            else:
                weight = 2.0
            energy = energy + weight * part
        energy_ref[...] = jnp.broadcast_to(energy, energy_ref.shape)
        send_ref[...] = staging[...].reshape(send_ref.shape).astype(jnp.bfloat16)


def exchange_kernel(n, degree, send_ref, energy_ref, orders_ref, recv_ref, basis_ref, total_ref, energies, send_sem, recv_sem, esend_sem, erecv_sem, own_sem):
    me = lax.axis_index("blk")
    barrier = pltpu.get_barrier_semaphore()

    def signal(s, carry):
        pl.semaphore_signal(barrier, inc=1, device_id={"blk": lax.rem(me + s, n)}, device_id_type=MESH)
        return carry

    lax.fori_loop(1, n, signal, 0)
    pl.semaphore_wait(barrier, n - 1)

    def block_copy(s):
        peer = lax.rem(me + s, n)
        return pltpu.make_async_remote_copy(
            src_ref=send_ref.at[peer], dst_ref=recv_ref.at[me], send_sem=send_sem.at[s], recv_sem=recv_sem.at[s],
            device_id={"blk": peer}, device_id_type=MESH)

    def energy_copy(s):
        peer = lax.rem(me + s, n)
        return pltpu.make_async_remote_copy(
            src_ref=energy_ref, dst_ref=energies.at[s], send_sem=esend_sem.at[s], recv_sem=erecv_sem.at[s],
            device_id={"blk": peer}, device_id_type=MESH)

    def start(i, carry):
        s = i + 1
        if n % 2 == 0:
            s = n // 2 + (i % 2) * ((i + 1) // 2) - (1 - i % 2) * (i // 2)
        block_copy(s).start()
        return carry

    def start_energy(s, carry):
        energy_copy(s).start()
        return carry

    lax.fori_loop(0, n - 1, start, 0)
    lax.fori_loop(1, n, start_energy, 0)
    own = pltpu.make_async_copy(send_ref.at[me], recv_ref.at[me], own_sem)
    own.start()

    rows = basis_ref.shape[0]
    row_id = lax.broadcasted_iota(jnp.int32, (rows, LANES), 0)
    lane_id = lax.broadcasted_iota(jnp.int32, (rows, LANES), 1)
    width = orders_ref.shape[1]
    pair_row = lax.broadcasted_iota(jnp.int32, (rows, width), 0) // 4
    pair_lane = lax.broadcasted_iota(jnp.int32, (rows, width), 1)
    spread = jnp.where(pair_row == pair_lane, orders_ref[...].astype(jnp.float32), 0.0)
    low = jnp.broadcast_to(jnp.sum(spread, axis=1, keepdims=True), (rows, LANES)).astype(jnp.int32)
    order = jnp.where((row_id & 2) == 0, low, degree - low)
    scale = 2.0 * math.pi / NLON
    turn = (order * (LANES * lane_id) + (row_id & 1) * (NLON // 4)) & (NLON - 1)
    fine = (order * lane_id) & (NLON - 1)
    factor = jnp.where(order == 0, 1.0, 2.0)
    coarse_angle = turn.astype(jnp.float32) * scale
    fine_angle = fine.astype(jnp.float32) * scale
    cos_coarse, sin_coarse = factor * jnp.cos(coarse_angle), factor * jnp.sin(coarse_angle)
    cos_fine, sin_fine = jnp.cos(fine_angle), jnp.sin(fine_angle)
    for tile in range(NLON // LANES):
        values = cos_coarse[:, tile : tile + 1] * cos_fine - sin_coarse[:, tile : tile + 1] * sin_fine
        basis_ref[:, tile * LANES : (tile + 1) * LANES] = values.astype(jnp.bfloat16)

    def finish_energy(s, total):
        energy_copy(s).wait()
        return total + energies[s]

    total_ref[...] = lax.fori_loop(1, n, finish_energy, energy_ref[...])

    def finish(s, carry):
        block_copy(s).wait()
        return carry

    lax.fori_loop(1, n, finish, 0)
    own.wait()


def wave_kernel(scale, recv_ref, basis_ref, total_ref, out_ref, energy_ref, held):
    groups = recv_ref.shape[1]
    depth = basis_ref.shape[0]
    fields = out_ref.shape[1]
    for group in range(groups):
        values = recv_ref[:, group, :, :].astype(jnp.float32).reshape(depth, LANES)
        held[group * LANES : (group + 1) * LANES, :] = jnp.transpose(values).astype(jnp.bfloat16)
    width = min(NLON, NLON * LANES // depth)

    @pl.loop(0, NLON // width)
    def _(tile):
        columns = pl.ds(pl.multiple_of(tile * width, width), width)
        for cycle in range(out_ref.shape[0]):
            rows = held[cycle * fields : (cycle + 1) * fields, :]
            wave = jnp.dot(rows, basis_ref[:, columns], preferred_element_type=jnp.float32)
            out_ref[cycle, :, columns] = wave.astype(jnp.bfloat16)

    energy_ref[...] = (total_ref[0:1, :fields] + total_ref[0:1, fields:]) * scale


def shards(load_coef, legendre, slab_orders, cycle_rows):
    n = lax.axis_size("blk")
    pairs, slab_rows, streams = load_coef.shape
    fields = streams // 2
    lat_count = legendre.shape[2]
    cycle_count = lat_count // n
    per_tile = LANES // fields
    groups = cycle_count // per_tile
    kinds = 4 * pairs
    degree = slab_rows - 2
    packed_rows = slab_rows * pairs
    padded = -(-packed_rows // LANES) * LANES
    table = jnp.transpose(legendre, (1, 0, 2))
    coef = jnp.transpose(load_coef, (1, 0, 2))
    steps = 4
    block = lat_count // steps
    send, energy = pl.pallas_call(
        functools.partial(spectra_kernel, pairs),
        grid_spec=pltpu.PrefetchScalarGridSpec(
            num_scalar_prefetch=1,
            grid=(steps,),
            in_specs=[
                pl.BlockSpec((slab_rows, pairs, block), lambda s, o: (0, 0, s)),
                pl.BlockSpec((slab_rows, pairs, streams), lambda s, o: (0, 0, 0), pipeline_mode=pl.Buffered(1)),
                pl.BlockSpec((lat_count // LANES, LANES), lambda s, o: (0, 0), pipeline_mode=pl.Buffered(1)),
            ],
            out_specs=[
                pl.BlockSpec((n, groups, kinds, LANES), lambda s, o: (0, 0, 0, 0)),
                pl.BlockSpec((8, streams), lambda s, o: (0, 0)),
            ],
            scratch_shapes=[
                pltpu.VMEM((2 * pairs * streams, padded), jnp.bfloat16),
                pltpu.VMEM((2 * pairs * streams, lat_count), jnp.bfloat16),
                pltpu.VMEM((lat_count // LANES, 2 * pairs, LANES, streams), jnp.float32),
                pltpu.VMEM((n * groups * kinds, LANES), jnp.float32),
            ],
        ),
        out_shape=[
            jax.ShapeDtypeStruct((n, groups, kinds, LANES), jnp.bfloat16),
            jax.ShapeDtypeStruct((8, streams), jnp.float32),
        ],
        compiler_params=pltpu.CompilerParams(dimension_semantics=("arbitrary",)),
    )(slab_orders, table, coef, cycle_rows.reshape(lat_count // LANES, LANES))
    recv, basis, total = pl.pallas_call(
        functools.partial(exchange_kernel, n, degree),
        out_shape=[
            jax.ShapeDtypeStruct((n, groups, kinds, LANES), jnp.bfloat16),
            jax.ShapeDtypeStruct((n * kinds, NLON), jnp.bfloat16),
            jax.ShapeDtypeStruct((8, streams), jnp.float32),
        ],
        in_specs=[
            pl.BlockSpec(memory_space=pl.ANY),
            pl.BlockSpec(memory_space=pltpu.VMEM),
            pl.BlockSpec(memory_space=pltpu.VMEM),
        ],
        out_specs=[
            pl.BlockSpec(memory_space=pl.ANY),
            pl.BlockSpec(memory_space=pltpu.VMEM),
            pl.BlockSpec(memory_space=pltpu.VMEM),
        ],
        scratch_shapes=[
            pltpu.VMEM((n, 8, streams), jnp.float32),
            pltpu.SemaphoreType.DMA((n,)),
            pltpu.SemaphoreType.DMA((n,)),
            pltpu.SemaphoreType.DMA((n,)),
            pltpu.SemaphoreType.DMA((n,)),
            pltpu.SemaphoreType.DMA,
        ],
        compiler_params=pltpu.CompilerParams(collective_id=0, has_side_effects=True),
    )(send, energy, slab_orders.reshape(1, n * pairs))
    step_groups = min(4, groups)
    potential, mean_square = pl.pallas_call(
        functools.partial(wave_kernel, 1.0 / lat_count),
        grid=(groups // step_groups,),
        out_shape=[
            jax.ShapeDtypeStruct((cycle_count, fields, NLON), jnp.bfloat16),
            jax.ShapeDtypeStruct((1, fields), jnp.float32),
        ],
        in_specs=[
            pl.BlockSpec((n, step_groups, kinds, LANES), lambda s: (0, s, 0, 0)),
            pl.BlockSpec((n * kinds, NLON), lambda s: (0, 0), pipeline_mode=pl.Buffered(1)),
            pl.BlockSpec((8, streams), lambda s: (0, 0), pipeline_mode=pl.Buffered(1)),
        ],
        out_specs=[
            pl.BlockSpec((step_groups * per_tile, fields, NLON), lambda s: (s, 0, 0)),
            pl.BlockSpec((1, fields), lambda s: (0, 0)),
        ],
        scratch_shapes=[pltpu.VMEM((step_groups * LANES, n * kinds), jnp.bfloat16)],
        compiler_params=pltpu.CompilerParams(dimension_semantics=("arbitrary",)),
    )(recv, basis, total)
    return potential, mean_square.reshape(fields)


def solution(mesh):
    in_specs = (P("blk", None, "rep"), P("blk", None, None), P(), P())
    out_specs = (P("blk", "rep", None), P("rep"))
    return jax.shard_map(shards, mesh=mesh, in_specs=in_specs, out_specs=out_specs, check_vma=False)
```

profile of v0, /device:TPU:1, one launch (start us, length us, event | category | flops | bytes accessed | tf_op | source)
XLA Modules:
  0.0 85.5 jit_solution(2140534706320952431)
XLA Ops:
  0.6 12.3 %shard_map.59 = (bf16[128,4,8,128]{3,2,1,0:T(8,128)(2,1)}, f32[8,128]{1,0:T(8,128)}) custom-call(s32[256]{0:T(256)} %orders_ref.1, bf16[2049,2,1024]{2,1,0:T(2,128)(2,1)} %bitcast.5, bf16[2049,2,128]{2,1,0:T(2,128)(2,1)} %bitcast.6, s32[8,128]{1,0:T(8,128)} %bitcast.7), custom_call_target="tpu_custom_call" | custom-call | tf_op jit(solution)/shard_map/pallas_call | solution.py:193
  12.9 53.9 %shard_map.60 = (bf16[128,4,8,128]{3,2,1,0:T(8,128)(2,1)}, bf16[1024,4096]{1,0:T(8,128)(2,1)}, f32[8,128]{1,0:T(8,128)}) custom-call(bf16[128,4,8,128]{3,2,1,0:T(8,128)(2,1)} %get-tuple-element.9.send_ref, f32[8,128]{1,0:T(8,128)} %get-tuple-element.10.energy_ref, s32[1,256]{1,0:T(1,128)} %bitcast.8), custom_call_target="tpu_custom_call" | custom-call | tf_op jit(solution)/shard_map/pallas_call | solution.py:220
  66.8 18.7 %shard_map.61 = (bf16[8,64,4096]{2,1,0:T(8,128)(2,1)}, f32[1,64]{1,0:T(1,128)}) custom-call(bf16[128,4,8,128]{3,2,1,0:T(8,128)(2,1)} %get-tuple-element.11.recv_ref, bf16[1024,4096]{1,0:T(8,128)(2,1)} %get-tuple-element.12.basis_ref, f32[8,128]{1,0:T(8,128)} %get-tuple-element.13.total_ref), custom_call_target="tpu_custom_call" | custom-call | tf_op jit(solution)/shard_map/pallas_call | solution.py:248
where the time goes:
time: 86.6 us; the launch traced here: 85.5 us
  Pallas kernels  84.8 us (98%)
    pallas_call x1, Pallas kernels, shards(): pl.pallas_call(functools.partial(exchange_kernel, n, degree), out_shape=[...  53.9 us
    pallas_call x1, Pallas kernels, shards(): pl.pallas_call(functools.partial(wave_kernel, 1.0 / lat_count), grid=(gro...  18.7 us
    pallas_call x1, Pallas kernels, shards(): pl.pallas_call(functools.partial(spectra_kernel, pairs), grid_spec=pltpu....  12.3 us

commit v1 on v0

v1 whole, which is shorter than its diff:
```python
import functools
import math

import jax
import jax.numpy as jnp
from jax import lax
from jax.experimental import pallas as pl
from jax.experimental.pallas import tpu as pltpu
from jax.sharding import PartitionSpec as P

NLON = 4096
HALF = NLON // 2
LANES = 128
MESH = pl.DeviceIdType.MESH
PLANES = 4
SPOTS = 16
CORES = 2
PER_PLANE = SPOTS * CORES
COLUMN = PLANES * CORES
HOPS = (2, 1, 3, 0)


def even_order(low, degree):
    return jnp.where((low & 1) == 0, low, degree - low)


def exchange_kernel(
    table_hbm, coef_hbm, rows_hbm, orders_hbm,
    held_ref, basis_ref, total_ref,
    table, coef, rows_v, orders_v, masked, chosen, spectra, send, recv, wide, partial, near, far,
    in_sem, table_sem, ready_sem, send_sem, recv_sem, near_send, near_recv, far_send, far_recv,
):
    slab_rows, pairs, lat_count = table_hbm.shape
    blocks = table.shape[0]
    block = table.shape[3]
    packed_rows = slab_rows * pairs
    degree = slab_rows - 2
    streams = coef.shape[2]
    fields = streams // 2
    n = PLANES * PER_PLANE
    per_peer = 2 * (lat_count // n)
    cycles = lat_count // n
    plane_rows = PER_PLANE * per_peer

    me = lax.axis_index("blk")
    plane = me // PER_PLANE
    inside = me % PER_PLANE
    spot = inside // CORES
    core = me % CORES

    coef_copy = pltpu.make_async_copy(coef_hbm, coef, in_sem.at[0])
    rows_copy = pltpu.make_async_copy(rows_hbm, rows_v, in_sem.at[1])
    orders_copy = pltpu.make_async_copy(orders_hbm, orders_v, in_sem.at[2])

    def table_copy(b):
        return pltpu.make_async_copy(table_hbm.at[:, :, pl.ds(pl.multiple_of(b * block, block), block)], table.at[b], table_sem.at[b])

    rows_copy.start()
    orders_copy.start()
    coef_copy.start()
    for b in range(blocks):
        table_copy(b).start()

    def column_peer(j):
        q = lax.rem(plane * CORES + core + j, COLUMN)
        return (q // CORES) * PER_PLANE + spot * CORES + q % CORES

    def spot_peer(j):
        return plane * PER_PLANE + lax.rem(spot + j, SPOTS) * CORES + core

    barrier = pltpu.get_barrier_semaphore()

    @pl.loop(1, COLUMN)
    def _(j):
        pl.semaphore_signal(barrier, inc=1, device_id={"blk": column_peer(j)}, device_id_type=MESH)

    @pl.loop(1, SPOTS)
    def _(j):
        pl.semaphore_signal(barrier, inc=1, device_id={"blk": spot_peer(j)}, device_id_type=MESH)

    rows_copy.wait()
    orders_copy.wait()
    columns = jnp.transpose(jnp.broadcast_to(rows_v[...].astype(jnp.float32)[None], (LANES // 8, 8, LANES)).reshape(LANES, LANES))
    cycle_id = lax.broadcasted_iota(jnp.int32, (LANES, lat_count), 1).astype(jnp.float32)
    for part in range(lat_count // LANES):
        chosen[part * LANES : (part + 1) * LANES, :] = (columns[:, part : part + 1] == cycle_id).astype(jnp.float32).astype(jnp.bfloat16)
    orders_row = orders_v[...]
    slot_id = lax.broadcasted_iota(jnp.int32, orders_row.shape, 1)
    lows = [jnp.sum(jnp.where(slot_id == me * pairs + p, orders_row, 0).astype(jnp.float32), axis=1, keepdims=True).astype(jnp.int32) for p in range(pairs)]

    coef_copy.wait()
    packed = coef[...].reshape(packed_rows, streams)
    padding = jnp.zeros((masked.shape[1] - packed_rows, streams), packed.dtype)
    flipped = jnp.transpose(jnp.concatenate([packed, padding], axis=0).astype(jnp.float32))
    packed_id = lax.broadcasted_iota(jnp.int32, (1, masked.shape[1]), 1)
    row_id = packed_id // pairs
    pair_id = packed_id % pairs
    for p in range(pairs):
        lower = (row_id < slab_rows - 1 - lows[p]).astype(jnp.int32)
        is_even = ((lows[p] & 1) == 0).astype(jnp.int32)
        in_even = (lower == is_even).astype(jnp.int32)
        for eo in range(2):
            keep = jnp.where(pair_id == p, jnp.where(in_even == 1 - eo, 1.0, 0.0), 0.0)
            start = (2 * p + eo) * streams
            masked[start : start + streams, :] = jnp.where(jnp.broadcast_to(keep, flipped.shape) > 0.5, flipped, 0.0).astype(jnp.bfloat16)

    pl.semaphore_wait(barrier, COLUMN - 1 + SPOTS - 1)

    @pl.loop(1, SPOTS)
    def _(j):
        pl.semaphore_signal(ready_sem, inc=1, device_id={"blk": spot_peer(j)}, device_id_type=MESH)

    def spectra_of(p, first):
        rows = slice(p * 2 * streams, (p + 1) * 2 * streams)

        @pl.loop(0, blocks)
        def _(b):
            if first:
                table_copy(b).wait()
            product = jnp.dot(masked[rows, :packed_rows], table[b].reshape(packed_rows, block), preferred_element_type=jnp.float32)
            spectra[rows, pl.ds(pl.multiple_of(b * block, block), block)] = product.astype(jnp.bfloat16)

    def sort_plane(p, target):
        count = PER_PLANE * cycles
        picked = chosen[pl.ds(pl.multiple_of(target * count, count), count), :]
        rows = lax.dot_general(picked, spectra[p * 2 * streams : (p + 1) * 2 * streams, :], (((1,), (1,)), ((), ())), preferred_element_type=jnp.float32)
        parts = [rows[:, eo * streams : (eo + 1) * streams].reshape(PER_PLANE, 1, cycles, streams) for eo in range(2)]
        message = jnp.concatenate(parts, axis=1).reshape(plane_rows, streams)
        send[p, pl.ds(pl.multiple_of(target * plane_rows, plane_rows), plane_rows), :] = message.astype(jnp.bfloat16)
        return jnp.sum(rows * rows, axis=0, keepdims=True)

    def block_rows(q):
        return pl.ds(pl.multiple_of(q * per_peer, per_peer), per_peer)

    def send_plane(p, hop):
        target = lax.rem(plane + hop, PLANES)

        @pl.loop(1 if hop == 0 else 0, PER_PLANE)
        def _(i):
            peer = target * PER_PLANE + lax.rem(spot + i // CORES, SPOTS) * CORES + lax.rem(core + i, CORES)
            pltpu.make_async_remote_copy(
                src_ref=send.at[p, block_rows(peer), :], dst_ref=recv.at[p, block_rows(me), :],
                send_sem=send_sem.at[p], recv_sem=recv_sem.at[p],
                device_id={"blk": peer}, device_id_type=MESH).start()

    def all_blocks(p):
        whole = pl.ds(0, (n - 1) * per_peer)
        return pltpu.make_async_remote_copy(
            src_ref=send.at[p, whole, :], dst_ref=recv.at[p, whole, :], send_sem=send_sem.at[p], recv_sem=recv_sem.at[p],
            device_id={"blk": column_peer(1)}, device_id_type=MESH)

    def keep_own(p):
        recv[p, block_rows(me), :] = send[p, block_rows(me), :]

    lane_id = lax.broadcasted_iota(jnp.int32, (1, streams), 1)

    def weighted(p, squares):
        even = even_order(lows[p], degree)
        out = jnp.zeros((1, streams), jnp.float32)
        for eo in range(2):
            order = even if eo == 0 else degree - even
            weight = jnp.where(order == 0, jnp.where(lane_id < fields, 1.0, 0.0), 2.0)
            out = out + weight * squares[:, eo * streams : (eo + 1) * streams]
        return out

    spectra_of(0, True)
    squares = sort_plane(0, lax.rem(plane + HOPS[0], PLANES))
    pl.semaphore_wait(ready_sem, SPOTS - 1)
    for i, hop in enumerate(HOPS):
        if i + 1 < PLANES:
            squares = squares + sort_plane(0, lax.rem(plane + HOPS[i + 1], PLANES))
        send_plane(0, hop)
    keep_own(0)
    energy = weighted(0, squares)

    for p in range(1, pairs):
        spectra_of(p, False)
        squares = sort_plane(p, plane)
        for hop in HOPS[:-1]:
            squares = squares + sort_plane(p, lax.rem(plane + hop, PLANES))
        keep_own(p)
        energy = energy + weighted(p, squares)
    partial[0] = energy

    def near_copy(j):
        return pltpu.make_async_remote_copy(
            src_ref=partial.at[0], dst_ref=near.at[j], send_sem=near_send.at[j], recv_sem=near_recv.at[j],
            device_id={"blk": column_peer(j)}, device_id_type=MESH)

    def far_copy(j):
        return pltpu.make_async_remote_copy(
            src_ref=partial.at[1], dst_ref=far.at[j], send_sem=far_send.at[j], recv_sem=far_recv.at[j],
            device_id={"blk": spot_peer(j)}, device_id_type=MESH)

    send_plane(1, HOPS[0])

    @pl.loop(1, COLUMN)
    def _(j):
        near_copy(j).start()

    for p in range(1, pairs):
        for hop in HOPS[1 if p == 1 else 0 :]:
            send_plane(p, hop)

    scale = 2.0 * math.pi / NLON
    source = lax.broadcasted_iota(jnp.int32, (n, n * pairs), 0)
    slot = lax.broadcasted_iota(jnp.int32, (n, n * pairs), 1)
    lane = lax.broadcasted_iota(jnp.int32, (n, LANES), 1)
    spread = jnp.broadcast_to(orders_row, (n, n * pairs)).astype(jnp.float32)

    @pl.loop(0, 2 * pairs)
    def _(item):
        p = item % pairs
        eo = item // pairs
        low = jnp.sum(jnp.where(slot == source * pairs + p, spread, 0.0), axis=1, keepdims=True).astype(jnp.int32)
        even = even_order(low, degree)
        order = jnp.where(eo == 0, even, degree - even)
        order = jnp.broadcast_to(order, (n, LANES))
        factor = jnp.where(order == 0, 1.0, 2.0)
        coarse_angle = ((order * (LANES * lane)) & (NLON - 1)).astype(jnp.float32) * scale
        fine_angle = ((order * lane) & (NLON - 1)).astype(jnp.float32) * scale
        cos_coarse, sin_coarse = factor * jnp.cos(coarse_angle), factor * jnp.sin(coarse_angle)
        cos_fine, sin_fine = jnp.cos(fine_angle), jnp.sin(fine_angle)
        first = pl.multiple_of(p * 2 * n, 2 * n)
        second = pl.multiple_of(p * 2 * n + n, n)
        for tile in range(HALF // LANES):
            cc, ss = cos_coarse[:, tile : tile + 1], sin_coarse[:, tile : tile + 1]
            lanes = slice(tile * LANES, (tile + 1) * LANES)
            basis_ref[eo, pl.ds(first, n), lanes] = (cc * cos_fine - ss * sin_fine).astype(jnp.bfloat16)
            basis_ref[eo, pl.ds(second, n), lanes] = (-(ss * cos_fine + cc * sin_fine)).astype(jnp.bfloat16)

    def finish(p):
        all_blocks(p).wait_recv()
        wide[...] = recv[p].astype(jnp.float32)
        for eo in range(2):
            for cycle in range(cycles):
                tile = jnp.transpose(wide[pl.ds(eo * cycles + cycle, n, stride=per_peer), :]).astype(jnp.bfloat16)
                rows = slice(cycle * fields, (cycle + 1) * fields)
                held_ref[eo, rows, p * 2 * n : p * 2 * n + n] = tile[:fields]
                held_ref[eo, rows, p * 2 * n + n : (p + 1) * 2 * n] = tile[fields:]

    finish(0)

    @pl.loop(1, COLUMN)
    def _(j):
        near_copy(j).wait()

    partial[1] = partial[0] + jnp.sum(near[1:], axis=0)

    @pl.loop(1, SPOTS)
    def _(j):
        far_copy(j).start()

    for p in range(1, pairs):
        finish(p)

    @pl.loop(1, SPOTS)
    def _(j):
        far_copy(j).wait()

    total_ref[...] = partial[1] + jnp.sum(far[1:], axis=0)
    for p in range(pairs):
        all_blocks(p).wait_send()


def wave_kernel(scale, held_ref, basis_ref, total_ref, out_hbm, energy_ref, out, out_sem):
    cycles, fields, _ = out.shape
    width = 256
    tiles = HALF // width

    def out_copy(tile, side):
        columns = pl.ds(pl.multiple_of(side * HALF + tile * width, width), width)
        return pltpu.make_async_copy(out.at[:, :, columns], out_hbm.at[:, :, columns], out_sem.at[tile, side])

    @pl.loop(0, tiles)
    def _(tile):
        columns = pl.ds(pl.multiple_of(tile * width, width), width)
        even = jnp.dot(held_ref[0], basis_ref[0, :, columns], preferred_element_type=jnp.float32)
        odd = jnp.dot(held_ref[1], basis_ref[1, :, columns], preferred_element_type=jnp.float32)
        out[:, :, columns] = (even + odd).astype(jnp.bfloat16).reshape(cycles, fields, width)
        mirrored = pl.ds(pl.multiple_of(HALF + tile * width, width), width)
        out[:, :, mirrored] = (even - odd).astype(jnp.bfloat16).reshape(cycles, fields, width)
        for side in range(2):
            out_copy(tile, side).start()

    energy_ref[...] = (total_ref[:, :fields] + total_ref[:, fields:]) * scale

    @pl.loop(0, tiles)
    def _(tile):
        for side in range(2):
            out_copy(tile, side).wait()


def shards(load_coef, legendre, slab_orders, cycle_rows):
    n = lax.axis_size("blk")
    pairs, slab_rows, streams = load_coef.shape
    fields = streams // 2
    lat_count = legendre.shape[2]
    cycles = lat_count // n
    packed_rows = slab_rows * pairs
    padded = -(-packed_rows // LANES) * LANES
    per_peer = 2 * cycles
    table = jnp.transpose(legendre, (1, 0, 2))
    coef = jnp.transpose(load_coef, (1, 0, 2))
    blocks = 4
    block = lat_count // blocks
    anywhere = pl.BlockSpec(memory_space=pltpu.HBM)
    vmem = pl.BlockSpec(memory_space=pltpu.VMEM)
    dma = pltpu.SemaphoreType.DMA
    held, basis, total = pl.pallas_call(
        exchange_kernel,
        out_shape=[
            jax.ShapeDtypeStruct((2, cycles * fields, pairs * 2 * n), jnp.bfloat16),
            jax.ShapeDtypeStruct((2, pairs * 2 * n, HALF), jnp.bfloat16),
            jax.ShapeDtypeStruct((1, streams), jnp.float32),
        ],
        in_specs=[anywhere] * 4,
        out_specs=[vmem] * 3,
        scratch_shapes=[
            pltpu.VMEM((blocks, slab_rows, pairs, block), jnp.bfloat16),
            pltpu.VMEM((slab_rows, pairs, streams), jnp.bfloat16),
            pltpu.VMEM((lat_count // LANES, LANES), jnp.int32),
            pltpu.VMEM((1, n * pairs), jnp.int32),
            pltpu.VMEM((2 * pairs * streams, padded), jnp.bfloat16),
            pltpu.VMEM((lat_count, lat_count), jnp.bfloat16),
            pltpu.VMEM((2 * pairs * streams, lat_count), jnp.bfloat16),
            pltpu.VMEM((pairs, n * per_peer, streams), jnp.bfloat16),
            pltpu.VMEM((pairs, n * per_peer, streams), jnp.bfloat16),
            pltpu.VMEM((n * per_peer, streams), jnp.float32),
            pltpu.VMEM((2, 1, streams), jnp.float32),
            pltpu.VMEM((COLUMN, 1, streams), jnp.float32),
            pltpu.VMEM((SPOTS, 1, streams), jnp.float32),
            dma((3,)),
            dma((blocks,)),
            pltpu.SemaphoreType.REGULAR,
            dma((pairs,)),
            dma((pairs,)),
            dma((COLUMN,)),
            dma((COLUMN,)),
            dma((SPOTS,)),
            dma((SPOTS,)),
        ],
        compiler_params=pltpu.CompilerParams(collective_id=0, has_side_effects=True, vmem_limit_bytes=44 * 2**20),
        name="exchange",
    )(table, coef, cycle_rows.reshape(lat_count // LANES, LANES), slab_orders.reshape(1, n * pairs))
    potential, mean_square = pl.pallas_call(
        functools.partial(wave_kernel, 1.0 / lat_count),
        out_shape=[
            jax.ShapeDtypeStruct((cycles, fields, NLON), jnp.bfloat16),
            jax.ShapeDtypeStruct((1, fields), jnp.float32),
        ],
        in_specs=[vmem] * 3,
        out_specs=[anywhere, vmem],
        scratch_shapes=[
            pltpu.VMEM((cycles, fields, NLON), jnp.bfloat16),
            dma((HALF // 256, 2)),
        ],
        compiler_params=pltpu.CompilerParams(vmem_limit_bytes=24 * 2**20),
        name="wave",
    )(held, basis, total)
    return potential, mean_square.reshape(fields)


def solution(mesh):
    in_specs = (P("blk", None, "rep"), P("blk", None, None), P(), P())
    out_specs = (P("blk", "rep", None), P("rep"))
    return jax.shard_map(shards, mesh=mesh, in_specs=in_specs, out_specs=out_specs, check_vma=False)
```

time: 86.6 us -> 48.4 us (0.56); the launches traced: 85.5 us -> 48.2 us
  Pallas kernels: 84.8 us -> 45 us
  local copies, waits for them, and re-layouts: 0 us -> 2.58 us
    pallas_call x3 -> x2, Pallas kernels: 84.8 us -> 45 us  [the longest x1 39.7 us: shards(): pl.pallas_call(exchange_kernel, out_shape=[jax.ShapeDtypeStruct((2, cycle...]
    unnamed x0 -> x6, local copies, waits for them, and re-layouts: none -> 2.58 us
where the time goes in v1:
time: 48.4 us; the launch traced here: 48.2 us
  Pallas kernels  45 us (93%)
  local copies, waits for them, and re-layouts  2.58 us (5%)
  between operations  0.65 us (1%)
    pallas_call x1, Pallas kernels, shards(): pl.pallas_call(exchange_kernel, out_shape=[jax.ShapeDtypeStruct((2, cycle...  39.7 us
    pallas_call x1, Pallas kernels, shards(): pl.pallas_call(functools.partial(wave_kernel, 1.0 / lat_count), out_shape...  5.31 us
    unnamed x6, local copies, waits for them, and re-layouts  2.58 us

profile of v1, /device:TPU:1, one launch (start us, length us, event | category | flops | bytes accessed | tf_op | source)
XLA Modules:
  0.0 48.2 jit_solution(6652225354730730571)
XLA Ops:
  0.6 0.0 copy-start
  0.6 1.2 %copy-done = bf16[2,2049,128]{2,0,1:T(2,128)(2,1)S(1)} copy-done((bf16[2,2049,128]{2,0,1:T(2,128)(2,1)S(1)}, bf16[2,2049,128]{2,0,1:T(2,128)(2,1)}, u32[]{:S(2)}) %copy-start) | copy-done | bytes 1049112
  1.9 0.0 copy-start.1
  1.9 0.7 %copy-done.1 = s32[1024]{0:T(1024)S(1)} copy-done((s32[1024]{0:T(1024)S(1)}, s32[1024]{0:T(1024)}, u32[]{:S(2)}) %copy-start.1) | copy-done | bytes 4120
  2.5 0.0 copy-start.2
  2.5 0.7 %copy-done.2 = s32[256]{0:T(256)S(1)} copy-done((s32[256]{0:T(256)S(1)}, s32[256]{0:T(256)}, u32[]{:S(2)}) %copy-start.2) | copy-done | bytes 1048
  3.2 39.7 %exchange.1 = (bf16[2,512,512]{2,1,0:T(8,128)(2,1)S(1)}, bf16[2,512,2048]{2,1,0:T(8,128)(2,1)S(1)}, f32[1,128]{1,0:T(1,128)S(1)}) custom-call(bf16[2049,2,1024]{2,1,0:T(2,128)(2,1)} %bitcast.8, bf16[2049,2,128]{2,1,0:T(2,128)(2,1)S(1)} %bitcast.5, s32[8,128]{1,0:T(8,128)S(1)} %bitcast.6, s32[1,256]{1,0:T(1,128)S(1)} %bitcast.7), custom_call_target="tpu_custom_call" | custom-call | tf_op jit(solution)/shard_map/exchange/pallas_call | solution.py:310
  42.9 5.3 %wave.1 = (bf16[8,64,4096]{2,1,0:T(8,128)(2,1)}, f32[1,64]{1,0:T(1,128)}) custom-call(bf16[2,512,512]{2,1,0:T(8,128)(2,1)S(1)} %get-tuple-element.7.held_ref, bf16[2,512,2048]{2,1,0:T(8,128)(2,1)S(1)} %get-tuple-element.8.basis_ref, f32[1,128]{1,0:T(1,128)S(1)} %get-tuple-element.9.total_ref), custom_call_target="tpu_custom_call" | custom-call | tf_op jit(solution)/shard_map/wave/pallas_call | solution.py:346
Async XLA Ops:
  0.6 1.2 %copy-start = (bf16[2,2049,128]{2,0,1:T(2,128)(2,1)S(1)}, bf16[2,2049,128]{2,0,1:T(2,128)(2,1)}, u32[]{:S(2)}) copy-start(bf16[2,2049,128]{2,0,1:T(2,128)(2,1)} %param.4) | copy-start | bytes 3147268
  1.9 0.7 %copy-start.1 = (s32[1024]{0:T(1024)S(1)}, s32[1024]{0:T(1024)}, u32[]{:S(2)}) copy-start(s32[1024]{0:T(1024)} %param.7) | copy-start | bytes 12292
  2.5 0.7 %copy-start.2 = (s32[256]{0:T(256)S(1)}, s32[256]{0:T(256)}, u32[]{:S(2)}) copy-start(s32[256]{0:T(256)} %param.6) | copy-start | bytes 3076

commit v2 on v1

--- a/solution.py
+++ b/solution.py
@@ -26,14 +26,15 @@
 
 def exchange_kernel(
     table_hbm, coef_hbm, rows_hbm, orders_hbm,
-    held_ref, basis_ref, total_ref,
-    table, coef, rows_v, orders_v, masked, chosen, spectra, send, recv, wide, partial, near, far,
+    sum_ref, held_ref, basis_ref, total_ref,
+    table, coef, rows_v, orders_v, masked, extra, chosen, spectra, send, recv, wide, partial, near, far, held_first, basis_first,
     in_sem, table_sem, ready_sem, send_sem, recv_sem, near_send, near_recv, far_send, far_recv,
 ):
     slab_rows, pairs, lat_count = table_hbm.shape
     blocks = table.shape[0]
     block = table.shape[3]
-    packed_rows = slab_rows * pairs
+    deep = masked.shape[1]
+    last = slab_rows - 1
     degree = slab_rows - 2
     streams = coef.shape[2]
     fields = streams // 2
@@ -58,8 +59,6 @@
     rows_copy.start()
     orders_copy.start()
     coef_copy.start()
-    for b in range(blocks):
-        table_copy(b).start()
 
     def column_peer(j):
         q = lax.rem(plane * CORES + core + j, COLUMN)
@@ -73,6 +72,9 @@
     @pl.loop(1, COLUMN)
     def _(j):
         pl.semaphore_signal(barrier, inc=1, device_id={"blk": column_peer(j)}, device_id_type=MESH)
+
+    for b in range(blocks):
+        table_copy(b).start()
 
     @pl.loop(1, SPOTS)
     def _(j):
@@ -89,21 +91,25 @@
     lows = [jnp.sum(jnp.where(slot_id == me * pairs + p, orders_row, 0).astype(jnp.float32), axis=1, keepdims=True).astype(jnp.int32) for p in range(pairs)]
 
     coef_copy.wait()
-    packed = coef[...].reshape(packed_rows, streams)
-    padding = jnp.zeros((masked.shape[1] - packed_rows, streams), packed.dtype)
-    flipped = jnp.transpose(jnp.concatenate([packed, padding], axis=0).astype(jnp.float32))
-    packed_id = lax.broadcasted_iota(jnp.int32, (1, masked.shape[1]), 1)
+    flipped = jnp.transpose(coef[:last].reshape(deep, streams))
+    tail = coef[last].astype(jnp.float32)
+    tail = jnp.transpose(jnp.concatenate([tail, jnp.zeros((8 - pairs, streams), jnp.float32)], axis=0))
+    packed_id = lax.broadcasted_iota(jnp.int32, (1, deep), 1)
     row_id = packed_id // pairs
     pair_id = packed_id % pairs
-    for p in range(pairs):
-        lower = (row_id < slab_rows - 1 - lows[p]).astype(jnp.int32)
-        is_even = ((lows[p] & 1) == 0).astype(jnp.int32)
-        in_even = (lower == is_even).astype(jnp.int32)
+
+    def mask(p):
+        is_even = (lows[p] & 1) == 0
+        lower = jnp.where(row_id < last - lows[p], 1, 0)
+        in_even = lower == jnp.where(is_even, 1, 0)
         for eo in range(2):
-            keep = jnp.where(pair_id == p, jnp.where(in_even == 1 - eo, 1.0, 0.0), 0.0)
+            keep = jnp.where(pair_id == p, jnp.where(in_even, 1.0 - eo, 1.0 * eo), 0.0).astype(jnp.bfloat16)
             start = (2 * p + eo) * streams
-            masked[start : start + streams, :] = jnp.where(jnp.broadcast_to(keep, flipped.shape) > 0.5, flipped, 0.0).astype(jnp.bfloat16)
-
+            masked[start : start + streams, :] = flipped * jnp.broadcast_to(keep, flipped.shape)
+            mine = jnp.where(is_even, 1.0 * eo, 1.0 - eo)
+            extra[start : start + streams, :] = jnp.broadcast_to(tail[:, p : p + 1] * mine, (streams, LANES))
+
+    mask(0)
     pl.semaphore_wait(barrier, COLUMN - 1 + SPOTS - 1)
 
     @pl.loop(1, SPOTS)
@@ -117,7 +123,9 @@
         def _(b):
             if first:
                 table_copy(b).wait()
-            product = jnp.dot(masked[rows, :packed_rows], table[b].reshape(packed_rows, block), preferred_element_type=jnp.float32)
+            product = jnp.dot(masked[rows, :], table[b, :last].reshape(deep, block), preferred_element_type=jnp.float32)
+            row = table[b, last].astype(jnp.float32)[p : p + 1, :]
+            product = product + jnp.concatenate([extra[rows, :]] * (block // LANES), axis=1) * row
             spectra[rows, pl.ds(pl.multiple_of(b * block, block), block)] = product.astype(jnp.bfloat16)
 
     def sort_plane(p, target):
@@ -166,12 +174,13 @@
     spectra_of(0, True)
     squares = sort_plane(0, lax.rem(plane + HOPS[0], PLANES))
     pl.semaphore_wait(ready_sem, SPOTS - 1)
-    for i, hop in enumerate(HOPS):
-        if i + 1 < PLANES:
-            squares = squares + sort_plane(0, lax.rem(plane + HOPS[i + 1], PLANES))
+    send_plane(0, HOPS[0])
+    for hop in HOPS[1:]:
+        squares = squares + sort_plane(0, lax.rem(plane + hop, PLANES))
         send_plane(0, hop)
     keep_own(0)
     energy = weighted(0, squares)
+    mask(1)
 
     for p in range(1, pairs):
         spectra_of(p, False)
@@ -192,15 +201,12 @@
             src_ref=partial.at[1], dst_ref=far.at[j], send_sem=far_send.at[j], recv_sem=far_recv.at[j],
             device_id={"blk": spot_peer(j)}, device_id_type=MESH)
 
+    @pl.loop(1, COLUMN)
+    def _(j):
+        near_copy(j).start()
+
     send_plane(1, HOPS[0])
-
-    @pl.loop(1, COLUMN)
-    def _(j):
-        near_copy(j).start()
-
-    for p in range(1, pairs):
-        for hop in HOPS[1 if p == 1 else 0 :]:
-            send_plane(p, hop)
+    send_plane(1, HOPS[1])
 
     scale = 2.0 * math.pi / NLON
     source = lax.broadcasted_iota(jnp.int32, (n, n * pairs), 0)
@@ -208,10 +214,7 @@
     lane = lax.broadcasted_iota(jnp.int32, (n, LANES), 1)
     spread = jnp.broadcast_to(orders_row, (n, n * pairs)).astype(jnp.float32)
 
-    @pl.loop(0, 2 * pairs)
-    def _(item):
-        p = item % pairs
-        eo = item // pairs
+    def fill_basis(p, out, eo):
         low = jnp.sum(jnp.where(slot == source * pairs + p, spread, 0.0), axis=1, keepdims=True).astype(jnp.int32)
         even = even_order(low, degree)
         order = jnp.where(eo == 0, even, degree - even)
@@ -221,38 +224,52 @@
         fine_angle = ((order * lane) & (NLON - 1)).astype(jnp.float32) * scale
         cos_coarse, sin_coarse = factor * jnp.cos(coarse_angle), factor * jnp.sin(coarse_angle)
         cos_fine, sin_fine = jnp.cos(fine_angle), jnp.sin(fine_angle)
-        first = pl.multiple_of(p * 2 * n, 2 * n)
-        second = pl.multiple_of(p * 2 * n + n, n)
         for tile in range(HALF // LANES):
             cc, ss = cos_coarse[:, tile : tile + 1], sin_coarse[:, tile : tile + 1]
             lanes = slice(tile * LANES, (tile + 1) * LANES)
-            basis_ref[eo, pl.ds(first, n), lanes] = (cc * cos_fine - ss * sin_fine).astype(jnp.bfloat16)
-            basis_ref[eo, pl.ds(second, n), lanes] = (-(ss * cos_fine + cc * sin_fine)).astype(jnp.bfloat16)
-
-    def finish(p):
+            out[eo, :n, lanes] = (cc * cos_fine - ss * sin_fine).astype(jnp.bfloat16)
+            out[eo, n:, lanes] = (-(ss * cos_fine + cc * sin_fine)).astype(jnp.bfloat16)
+
+    @pl.loop(0, 2)
+    def _(eo):
+        fill_basis(0, basis_first, eo)
+
+    @pl.loop(1, COLUMN)
+    def _(j):
+        near_copy(j).wait()
+
+    partial[1] = partial[0] + jnp.sum(near[1:], axis=0)
+
+    @pl.loop(1, SPOTS)
+    def _(j):
+        far_copy(j).start()
+
+    send_plane(1, HOPS[2])
+    send_plane(1, HOPS[3])
+
+    @pl.loop(0, 2)
+    def _(eo):
+        fill_basis(1, basis_ref, eo)
+
+    def finish(p, out):
         all_blocks(p).wait_recv()
         wide[...] = recv[p].astype(jnp.float32)
         for eo in range(2):
             for cycle in range(cycles):
                 tile = jnp.transpose(wide[pl.ds(eo * cycles + cycle, n, stride=per_peer), :]).astype(jnp.bfloat16)
                 rows = slice(cycle * fields, (cycle + 1) * fields)
-                held_ref[eo, rows, p * 2 * n : p * 2 * n + n] = tile[:fields]
-                held_ref[eo, rows, p * 2 * n + n : (p + 1) * 2 * n] = tile[fields:]
-
-    finish(0)
-
-    @pl.loop(1, COLUMN)
-    def _(j):
-        near_copy(j).wait()
-
-    partial[1] = partial[0] + jnp.sum(near[1:], axis=0)
-
-    @pl.loop(1, SPOTS)
-    def _(j):
-        far_copy(j).start()
-
-    for p in range(1, pairs):
-        finish(p)
+                out[eo, rows, :n] = tile[:fields]
+                out[eo, rows, n:] = tile[fields:]
+
+    finish(0, held_first)
+
+    @pl.loop(0, HALF // block)
+    def _(tile):
+        lanes = pl.ds(pl.multiple_of(tile * block, block), block)
+        for eo in range(2):
+            sum_ref[eo, :, lanes] = jnp.dot(held_first[eo], basis_first[eo, :, lanes], preferred_element_type=jnp.float32)
+
+    finish(1, held_ref)
 
     @pl.loop(1, SPOTS)
     def _(j):
@@ -263,7 +280,7 @@
         all_blocks(p).wait_send()
 
 
-def wave_kernel(scale, held_ref, basis_ref, total_ref, out_hbm, energy_ref, out, out_sem):
+def wave_kernel(scale, sum_ref, held_ref, basis_ref, total_ref, out_hbm, energy_ref, out, out_sem):
     cycles, fields, _ = out.shape
     width = 256
     tiles = HALF // width
@@ -272,11 +289,11 @@
         columns = pl.ds(pl.multiple_of(side * HALF + tile * width, width), width)
         return pltpu.make_async_copy(out.at[:, :, columns], out_hbm.at[:, :, columns], out_sem.at[tile, side])
 
-    @pl.loop(0, tiles)
+    @pl.loop(0, tiles, unroll=8)
     def _(tile):
         columns = pl.ds(pl.multiple_of(tile * width, width), width)
-        even = jnp.dot(held_ref[0], basis_ref[0, :, columns], preferred_element_type=jnp.float32)
-        odd = jnp.dot(held_ref[1], basis_ref[1, :, columns], preferred_element_type=jnp.float32)
+        even = sum_ref[0, :, columns] + jnp.dot(held_ref[0], basis_ref[0, :, columns], preferred_element_type=jnp.float32)
+        odd = sum_ref[1, :, columns] + jnp.dot(held_ref[1], basis_ref[1, :, columns], preferred_element_type=jnp.float32)
         out[:, :, columns] = (even + odd).astype(jnp.bfloat16).reshape(cycles, fields, width)
         mirrored = pl.ds(pl.multiple_of(HALF + tile * width, width), width)
         out[:, :, mirrored] = (even - odd).astype(jnp.bfloat16).reshape(cycles, fields, width)
@@ -297,8 +314,7 @@
     fields = streams // 2
     lat_count = legendre.shape[2]
     cycles = lat_count // n
-    packed_rows = slab_rows * pairs
-    padded = -(-packed_rows // LANES) * LANES
+    deep = (slab_rows - 1) * pairs
     per_peer = 2 * cycles
     table = jnp.transpose(legendre, (1, 0, 2))
     coef = jnp.transpose(load_coef, (1, 0, 2))
@@ -307,21 +323,23 @@
     anywhere = pl.BlockSpec(memory_space=pltpu.HBM)
     vmem = pl.BlockSpec(memory_space=pltpu.VMEM)
     dma = pltpu.SemaphoreType.DMA
-    held, basis, total = pl.pallas_call(
+    first, held, basis, total = pl.pallas_call(
         exchange_kernel,
         out_shape=[
-            jax.ShapeDtypeStruct((2, cycles * fields, pairs * 2 * n), jnp.bfloat16),
-            jax.ShapeDtypeStruct((2, pairs * 2 * n, HALF), jnp.bfloat16),
+            jax.ShapeDtypeStruct((2, cycles * fields, HALF), jnp.float32),
+            jax.ShapeDtypeStruct((2, cycles * fields, 2 * n), jnp.bfloat16),
+            jax.ShapeDtypeStruct((2, 2 * n, HALF), jnp.bfloat16),
             jax.ShapeDtypeStruct((1, streams), jnp.float32),
         ],
         in_specs=[anywhere] * 4,
-        out_specs=[vmem] * 3,
+        out_specs=[vmem] * 4,
         scratch_shapes=[
             pltpu.VMEM((blocks, slab_rows, pairs, block), jnp.bfloat16),
             pltpu.VMEM((slab_rows, pairs, streams), jnp.bfloat16),
             pltpu.VMEM((lat_count // LANES, LANES), jnp.int32),
             pltpu.VMEM((1, n * pairs), jnp.int32),
-            pltpu.VMEM((2 * pairs * streams, padded), jnp.bfloat16),
+            pltpu.VMEM((2 * pairs * streams, deep), jnp.bfloat16),
+            pltpu.VMEM((2 * pairs * streams, LANES), jnp.float32),
             pltpu.VMEM((lat_count, lat_count), jnp.bfloat16),
             pltpu.VMEM((2 * pairs * streams, lat_count), jnp.bfloat16),
             pltpu.VMEM((pairs, n * per_peer, streams), jnp.bfloat16),
@@ -330,6 +348,8 @@
             pltpu.VMEM((2, 1, streams), jnp.float32),
             pltpu.VMEM((COLUMN, 1, streams), jnp.float32),
             pltpu.VMEM((SPOTS, 1, streams), jnp.float32),
+            pltpu.VMEM((2, cycles * fields, 2 * n), jnp.bfloat16),
+            pltpu.VMEM((2, 2 * n, HALF), jnp.bfloat16),
             dma((3,)),
             dma((blocks,)),
             pltpu.SemaphoreType.REGULAR,
@@ -340,16 +360,16 @@
             dma((SPOTS,)),
             dma((SPOTS,)),
         ],
-        compiler_params=pltpu.CompilerParams(collective_id=0, has_side_effects=True, vmem_limit_bytes=44 * 2**20),
+        compiler_params=pltpu.CompilerParams(collective_id=0, has_side_effects=True, vmem_limit_bytes=36 * 2**20),
         name="exchange",
-    )(table, coef, cycle_rows.reshape(lat_count // LANES, LANES), slab_orders.reshape(1, n * pairs))
+    )(*[pltpu.with_memory_space_constraint(x, pltpu.HBM) for x in (table, coef, cycle_rows.reshape(lat_count // LANES, LANES), slab_orders.reshape(1, n * pairs))])
     potential, mean_square = pl.pallas_call(
         functools.partial(wave_kernel, 1.0 / lat_count),
         out_shape=[
             jax.ShapeDtypeStruct((cycles, fields, NLON), jnp.bfloat16),
             jax.ShapeDtypeStruct((1, fields), jnp.float32),
         ],
-        in_specs=[vmem] * 3,
+        in_specs=[vmem] * 4,
         out_specs=[anywhere, vmem],
         scratch_shapes=[
             pltpu.VMEM((cycles, fields, NLON), jnp.bfloat16),
@@ -357,7 +377,7 @@
         ],
         compiler_params=pltpu.CompilerParams(vmem_limit_bytes=24 * 2**20),
         name="wave",
-    )(held, basis, total)
+    )(first, held, basis, total)
     return potential, mean_square.reshape(fields)
 
 

time: 48.4 us -> 44.7 us (0.924)
  local copies, waits for them, and re-layouts: 2.58 us -> 0 us
  Pallas kernels: 45 us -> 44 us
    unnamed x6 -> x0, local copies, waits for them, and re-layouts: 2.58 us -> none
    pallas_call x1, Pallas kernels: 5.31 us -> 2.96 us  [shards(): pl.pallas_call(functools.partial(wave_kernel, 1.0 / lat_count), out_shape...]
    pallas_call x1, Pallas kernels: 39.7 us -> 41 us  [shards(): pl.pallas_call(exchange_kernel, out_shape=[jax.ShapeDtypeStruct((2, cycle...]
where the time goes in v2:
time: 44.7 us; the launch traced here: 44.6 us
  Pallas kernels  44 us (98%)
  between operations  0.64 us (1%)
    pallas_call x1, Pallas kernels, shards(): pl.pallas_call(exchange_kernel, out_shape=[jax.ShapeDtypeStruct((2, cycle...  41 us
    pallas_call x1, Pallas kernels, shards(): pl.pallas_call(functools.partial(wave_kernel, 1.0 / lat_count), out_shape...  2.96 us

profile of v2, /device:TPU:1, one launch (start us, length us, event | category | flops | bytes accessed | tf_op | source)
XLA Modules:
  0.0 44.6 jit_solution(11217181814130210514)
XLA Ops:
  0.6 41.0 %exchange.1 = (f32[2,512,2048]{2,1,0:T(8,128)S(1)}, bf16[2,512,256]{2,1,0:T(8,128)(2,1)S(1)}, bf16[2,256,2048]{2,1,0:T(8,128)(2,1)S(1)}, f32[1,128]{1,0:T(1,128)S(1)}) custom-call(bf16[2049,2,1024]{2,1,0:T(2,128)(2,1)} %bitcast.5, bf16[2049,2,128]{2,1,0:T(2,128)(2,1)} %bitcast.6, s32[8,128]{1,0:T(8,128)} %bitcast.7, s32[1,256]{1,0:T(1,128)} %bitcast.8), custom_call_target="tpu_custom_call" | custom-call | tf_op jit(solution)/shard_map/exchange/pallas_call | solution.py:326
  41.7 3.0 %wave.1 = (bf16[8,64,4096]{2,1,0:T(8,128)(2,1)}, f32[1,64]{1,0:T(1,128)}) custom-call(f32[2,512,2048]{2,1,0:T(8,128)S(1)} %get-tuple-element.8.sum_ref, bf16[2,512,256]{2,1,0:T(8,128)(2,1)S(1)} %get-tuple-element.9.held_ref, bf16[2,256,2048]{2,1,0:T(8,128)(2,1)S(1)} %get-tuple-element.10.basis_ref, f32[1,128]{1,0:T(1,128)S(1)} %get-tuple-element.11.total_ref), custom_call_target="tpu_custom_call" | custom-call | tf_op jit(solution)/shard_map/wave/pallas_call | solution.py:366

commit v3 on v2

--- a/solution.py
+++ b/solution.py
@@ -27,12 +27,12 @@
 def exchange_kernel(
     table_hbm, coef_hbm, rows_hbm, orders_hbm,
     sum_ref, held_ref, basis_ref, total_ref,
-    table, coef, rows_v, orders_v, masked, extra, chosen, spectra, send, recv, wide, partial, near, far, held_first, basis_first,
+    table, table_last, coef, rows_v, orders_v, masked, extra, chosen, spectra, send, recv, wide, partial, near, far, held_first, basis_first,
     in_sem, table_sem, ready_sem, send_sem, recv_sem, near_send, near_recv, far_send, far_recv,
 ):
     slab_rows, pairs, lat_count = table_hbm.shape
     blocks = table.shape[0]
-    block = table.shape[3]
+    block = 2 * LANES
     deep = masked.shape[1]
     last = slab_rows - 1
     degree = slab_rows - 2
@@ -53,11 +53,15 @@
     rows_copy = pltpu.make_async_copy(rows_hbm, rows_v, in_sem.at[1])
     orders_copy = pltpu.make_async_copy(orders_hbm, orders_v, in_sem.at[2])
 
+    last_copy = pltpu.make_async_copy(table_hbm.at[pl.ds(last, 1)], table_last, in_sem.at[3])
+
     def table_copy(b):
-        return pltpu.make_async_copy(table_hbm.at[:, :, pl.ds(pl.multiple_of(b * block, block), block)], table.at[b], table_sem.at[b])
+        flat = table_hbm.reshape(slab_rows * pairs, lat_count)
+        return pltpu.make_async_copy(flat.at[pl.ds(0, deep), pl.ds(pl.multiple_of(b * LANES, LANES), LANES)], table.at[b], table_sem.at[b])
 
     rows_copy.start()
     orders_copy.start()
+    last_copy.start()
     coef_copy.start()
 
     def column_peer(j):
@@ -82,6 +86,7 @@
 
     rows_copy.wait()
     orders_copy.wait()
+    last_copy.wait()
     columns = jnp.transpose(jnp.broadcast_to(rows_v[...].astype(jnp.float32)[None], (LANES // 8, 8, LANES)).reshape(LANES, LANES))
     cycle_id = lax.broadcasted_iota(jnp.int32, (LANES, lat_count), 1).astype(jnp.float32)
     for part in range(lat_count // LANES):
@@ -119,12 +124,14 @@
     def spectra_of(p, first):
         rows = slice(p * 2 * streams, (p + 1) * 2 * streams)
 
-        @pl.loop(0, blocks)
+        @pl.loop(0, lat_count // block)
         def _(b):
             if first:
-                table_copy(b).wait()
-            product = jnp.dot(masked[rows, :], table[b, :last].reshape(deep, block), preferred_element_type=jnp.float32)
-            row = table[b, last].astype(jnp.float32)[p : p + 1, :]
+                table_copy(2 * b).wait()
+                table_copy(2 * b + 1).wait()
+            right = jnp.concatenate([table[2 * b + i] for i in range(2)], axis=1)
+            product = jnp.dot(masked[rows, :], right, preferred_element_type=jnp.float32)
+            row = table_last[0, :, pl.ds(pl.multiple_of(b * block, block), block)].astype(jnp.float32)[p : p + 1, :]
             product = product + jnp.concatenate([extra[rows, :]] * (block // LANES), axis=1) * row
             spectra[rows, pl.ds(pl.multiple_of(b * block, block), block)] = product.astype(jnp.bfloat16)
 
@@ -318,8 +325,7 @@
     per_peer = 2 * cycles
     table = jnp.transpose(legendre, (1, 0, 2))
     coef = jnp.transpose(load_coef, (1, 0, 2))
-    blocks = 4
-    block = lat_count // blocks
+    blocks = lat_count // LANES
     anywhere = pl.BlockSpec(memory_space=pltpu.HBM)
     vmem = pl.BlockSpec(memory_space=pltpu.VMEM)
     dma = pltpu.SemaphoreType.DMA
@@ -334,7 +340,8 @@
         in_specs=[anywhere] * 4,
         out_specs=[vmem] * 4,
         scratch_shapes=[
-            pltpu.VMEM((blocks, slab_rows, pairs, block), jnp.bfloat16),
+            pltpu.VMEM((blocks, deep, LANES), jnp.bfloat16),
+            pltpu.VMEM((1, pairs, lat_count), jnp.bfloat16),
             pltpu.VMEM((slab_rows, pairs, streams), jnp.bfloat16),
             pltpu.VMEM((lat_count // LANES, LANES), jnp.int32),
             pltpu.VMEM((1, n * pairs), jnp.int32),
@@ -350,7 +357,7 @@
             pltpu.VMEM((SPOTS, 1, streams), jnp.float32),
             pltpu.VMEM((2, cycles * fields, 2 * n), jnp.bfloat16),
             pltpu.VMEM((2, 2 * n, HALF), jnp.bfloat16),
-            dma((3,)),
+            dma((4,)),
             dma((blocks,)),
             pltpu.SemaphoreType.REGULAR,
             dma((pairs,)),

time: 44.7 us -> 44 us (0.984)
  Pallas kernels: 44 us -> 43.3 us
    pallas_call x1, Pallas kernels: 41 us -> 40.3 us  [shards(): pl.pallas_call(exchange_kernel, out_shape=[jax.ShapeDtypeStruct((2, cycle...]
where the time goes in v3:
time: 44 us; the launch traced here: 43.9 us
  Pallas kernels  43.3 us (98%)
  between operations  0.64 us (1%)
    pallas_call x1, Pallas kernels, shards(): pl.pallas_call(exchange_kernel, out_shape=[jax.ShapeDtypeStruct((2, cycle...  40.3 us
    pallas_call x1, Pallas kernels, shards(): pl.pallas_call(functools.partial(wave_kernel, 1.0 / lat_count), out_shape...  2.96 us

profile of v3, /device:TPU:1, one launch (start us, length us, event | category | flops | bytes accessed | tf_op | source)
XLA Modules:
  0.0 43.9 jit_solution(14755582852827403169)
XLA Ops:
  0.6 40.3 %exchange.1 = (f32[2,512,2048]{2,1,0:T(8,128)S(1)}, bf16[2,512,256]{2,1,0:T(8,128)(2,1)S(1)}, bf16[2,256,2048]{2,1,0:T(8,128)(2,1)S(1)}, f32[1,128]{1,0:T(1,128)S(1)}) custom-call(bf16[2049,2,1024]{2,1,0:T(2,128)(2,1)} %bitcast.5, bf16[2049,2,128]{2,1,0:T(2,128)(2,1)} %bitcast.6, s32[8,128]{1,0:T(8,128)} %bitcast.7, s32[1,256]{1,0:T(1,128)} %bitcast.8), custom_call_target="tpu_custom_call" | custom-call | tf_op jit(solution)/shard_map/exchange/pallas_call | solution.py:332
  40.9 3.0 %wave.1 = (bf16[8,64,4096]{2,1,0:T(8,128)(2,1)}, f32[1,64]{1,0:T(1,128)}) custom-call(f32[2,512,2048]{2,1,0:T(8,128)S(1)} %get-tuple-element.8.sum_ref, bf16[2,512,256]{2,1,0:T(8,128)(2,1)S(1)} %get-tuple-element.9.held_ref, bf16[2,256,2048]{2,1,0:T(8,128)(2,1)S(1)} %get-tuple-element.10.basis_ref, f32[1,128]{1,0:T(1,128)S(1)} %get-tuple-element.11.total_ref), custom_call_target="tpu_custom_call" | custom-call | tf_op jit(solution)/shard_map/wave/pallas_call | solution.py:373

commit v4 on v3

--- a/solution.py
+++ b/solution.py
@@ -27,7 +27,7 @@
 def exchange_kernel(
     table_hbm, coef_hbm, rows_hbm, orders_hbm,
     sum_ref, held_ref, basis_ref, total_ref,
-    table, table_last, coef, rows_v, orders_v, masked, extra, chosen, spectra, send, recv, wide, partial, near, far, held_first, basis_first,
+    table, table_last, coef, coef_last, rows_v, orders_v, masked, extra, chosen, spectra, send, recv, wide, partial, near, far, held_first, basis_first,
     in_sem, table_sem, ready_sem, send_sem, recv_sem, near_send, near_recv, far_send, far_recv,
 ):
     slab_rows, pairs, lat_count = table_hbm.shape
@@ -36,7 +36,7 @@
     deep = masked.shape[1]
     last = slab_rows - 1
     degree = slab_rows - 2
-    streams = coef.shape[2]
+    streams = coef.shape[1]
     fields = streams // 2
     n = PLANES * PER_PLANE
     per_peer = 2 * (lat_count // n)
@@ -49,7 +49,8 @@
     spot = inside // CORES
     core = me % CORES
 
-    coef_copy = pltpu.make_async_copy(coef_hbm, coef, in_sem.at[0])
+    coef_copy = pltpu.make_async_copy(coef_hbm.reshape(slab_rows * pairs, streams).at[pl.ds(0, deep)], coef, in_sem.at[0])
+    tail_copy = pltpu.make_async_copy(coef_hbm.at[pl.ds(last, 1)], coef_last, in_sem.at[4])
     rows_copy = pltpu.make_async_copy(rows_hbm, rows_v, in_sem.at[1])
     orders_copy = pltpu.make_async_copy(orders_hbm, orders_v, in_sem.at[2])
 
@@ -62,6 +63,7 @@
     rows_copy.start()
     orders_copy.start()
     last_copy.start()
+    tail_copy.start()
     coef_copy.start()
 
     def column_peer(j):
@@ -87,6 +89,7 @@
     rows_copy.wait()
     orders_copy.wait()
     last_copy.wait()
+    tail_copy.wait()
     columns = jnp.transpose(jnp.broadcast_to(rows_v[...].astype(jnp.float32)[None], (LANES // 8, 8, LANES)).reshape(LANES, LANES))
     cycle_id = lax.broadcasted_iota(jnp.int32, (LANES, lat_count), 1).astype(jnp.float32)
     for part in range(lat_count // LANES):
@@ -96,8 +99,8 @@
     lows = [jnp.sum(jnp.where(slot_id == me * pairs + p, orders_row, 0).astype(jnp.float32), axis=1, keepdims=True).astype(jnp.int32) for p in range(pairs)]
 
     coef_copy.wait()
-    flipped = jnp.transpose(coef[:last].reshape(deep, streams))
-    tail = coef[last].astype(jnp.float32)
+    flipped = jnp.transpose(coef[...])
+    tail = coef_last[0].astype(jnp.float32)
     tail = jnp.transpose(jnp.concatenate([tail, jnp.zeros((8 - pairs, streams), jnp.float32)], axis=0))
     packed_id = lax.broadcasted_iota(jnp.int32, (1, deep), 1)
     row_id = packed_id // pairs
@@ -200,20 +203,20 @@
 
     def near_copy(j):
         return pltpu.make_async_remote_copy(
-            src_ref=partial.at[0], dst_ref=near.at[j], send_sem=near_send.at[j], recv_sem=near_recv.at[j],
+            src_ref=partial.at[1], dst_ref=near.at[j], send_sem=near_send.at[j], recv_sem=near_recv.at[j],
             device_id={"blk": column_peer(j)}, device_id_type=MESH)
 
     def far_copy(j):
         return pltpu.make_async_remote_copy(
-            src_ref=partial.at[1], dst_ref=far.at[j], send_sem=far_send.at[j], recv_sem=far_recv.at[j],
+            src_ref=partial.at[0], dst_ref=far.at[j], send_sem=far_send.at[j], recv_sem=far_recv.at[j],
             device_id={"blk": spot_peer(j)}, device_id_type=MESH)
 
-    @pl.loop(1, COLUMN)
-    def _(j):
-        near_copy(j).start()
-
-    send_plane(1, HOPS[0])
-    send_plane(1, HOPS[1])
+    @pl.loop(1, SPOTS)
+    def _(j):
+        far_copy(j).start()
+
+    for hop in HOPS:
+        send_plane(1, hop)
 
     scale = 2.0 * math.pi / NLON
     source = lax.broadcasted_iota(jnp.int32, (n, n * pairs), 0)
@@ -241,18 +244,15 @@
     def _(eo):
         fill_basis(0, basis_first, eo)
 
+    @pl.loop(1, SPOTS)
+    def _(j):
+        far_copy(j).wait()
+
+    partial[1] = partial[0] + jnp.sum(far[1:], axis=0)
+
     @pl.loop(1, COLUMN)
     def _(j):
-        near_copy(j).wait()
-
-    partial[1] = partial[0] + jnp.sum(near[1:], axis=0)
-
-    @pl.loop(1, SPOTS)
-    def _(j):
-        far_copy(j).start()
-
-    send_plane(1, HOPS[2])
-    send_plane(1, HOPS[3])
+        near_copy(j).start()
 
     @pl.loop(0, 2)
     def _(eo):
@@ -278,11 +278,11 @@
 
     finish(1, held_ref)
 
-    @pl.loop(1, SPOTS)
-    def _(j):
-        far_copy(j).wait()
-
-    total_ref[...] = partial[1] + jnp.sum(far[1:], axis=0)
+    @pl.loop(1, COLUMN)
+    def _(j):
+        near_copy(j).wait()
+
+    total_ref[...] = partial[1] + jnp.sum(near[1:], axis=0)
     for p in range(pairs):
         all_blocks(p).wait_send()
 
@@ -342,7 +342,8 @@
         scratch_shapes=[
             pltpu.VMEM((blocks, deep, LANES), jnp.bfloat16),
             pltpu.VMEM((1, pairs, lat_count), jnp.bfloat16),
-            pltpu.VMEM((slab_rows, pairs, streams), jnp.bfloat16),
+            pltpu.VMEM((deep, streams), jnp.bfloat16),
+            pltpu.VMEM((1, pairs, streams), jnp.bfloat16),
             pltpu.VMEM((lat_count // LANES, LANES), jnp.int32),
             pltpu.VMEM((1, n * pairs), jnp.int32),
             pltpu.VMEM((2 * pairs * streams, deep), jnp.bfloat16),
@@ -357,7 +358,7 @@
             pltpu.VMEM((SPOTS, 1, streams), jnp.float32),
             pltpu.VMEM((2, cycles * fields, 2 * n), jnp.bfloat16),
             pltpu.VMEM((2, 2 * n, HALF), jnp.bfloat16),
-            dma((4,)),
+            dma((5,)),
             dma((blocks,)),
             pltpu.SemaphoreType.REGULAR,
             dma((pairs,)),

time: 44 us -> 40.8 us (0.927)
  Pallas kernels: 43.3 us -> 40 us
    pallas_call x1, Pallas kernels: 40.3 us -> 37.1 us  [shards(): pl.pallas_call(exchange_kernel, out_shape=[jax.ShapeDtypeStruct((2, cycle...]
where the time goes in v4:
time: 40.8 us; the launch traced here: 40.7 us
  Pallas kernels  40 us (98%)
  between operations  0.64 us (2%)
    pallas_call x1, Pallas kernels, shards(): pl.pallas_call(exchange_kernel, out_shape=[jax.ShapeDtypeStruct((2, cycle...  37.1 us
    pallas_call x1, Pallas kernels, shards(): pl.pallas_call(functools.partial(wave_kernel, 1.0 / lat_count), out_shape...  2.96 us

profile of v4, /device:TPU:1, one launch (start us, length us, event | category | flops | bytes accessed | tf_op | source)
XLA Modules:
  0.0 40.7 jit_solution(7642112524261580174)
XLA Ops:
  0.6 37.1 %exchange.1 = (f32[2,512,2048]{2,1,0:T(8,128)S(1)}, bf16[2,512,256]{2,1,0:T(8,128)(2,1)S(1)}, bf16[2,256,2048]{2,1,0:T(8,128)(2,1)S(1)}, f32[1,128]{1,0:T(1,128)S(1)}) custom-call(bf16[2049,2,1024]{2,1,0:T(2,128)(2,1)} %bitcast.5, bf16[2049,2,128]{2,1,0:T(2,128)(2,1)} %bitcast.6, s32[8,128]{1,0:T(8,128)} %bitcast.7, s32[1,256]{1,0:T(1,128)} %bitcast.8), custom_call_target="tpu_custom_call" | custom-call | tf_op jit(solution)/shard_map/exchange/pallas_call | solution.py:332
  37.7 3.0 %wave.1 = (bf16[8,64,4096]{2,1,0:T(8,128)(2,1)}, f32[1,64]{1,0:T(1,128)}) custom-call(f32[2,512,2048]{2,1,0:T(8,128)S(1)} %get-tuple-element.8.sum_ref, bf16[2,512,256]{2,1,0:T(8,128)(2,1)S(1)} %get-tuple-element.9.held_ref, bf16[2,256,2048]{2,1,0:T(8,128)(2,1)S(1)} %get-tuple-element.10.basis_ref, f32[1,128]{1,0:T(1,128)S(1)} %get-tuple-element.11.total_ref), custom_call_target="tpu_custom_call" | custom-call | tf_op jit(solution)/shard_map/wave/pallas_call | solution.py:374

commit v5 on v4

--- a/solution.py
+++ b/solution.py
@@ -260,10 +260,12 @@
 
     def finish(p, out):
         all_blocks(p).wait_recv()
-        wide[...] = recv[p].astype(jnp.float32)
+        arrived = recv[p].astype(jnp.float32).reshape(n, 2, cycles, streams)
+        for eo in range(2):
+            wide[eo] = arrived[:, eo].reshape(n * cycles, streams)
         for eo in range(2):
             for cycle in range(cycles):
-                tile = jnp.transpose(wide[pl.ds(eo * cycles + cycle, n, stride=per_peer), :]).astype(jnp.bfloat16)
+                tile = jnp.transpose(wide[eo, pl.ds(cycle, n, stride=cycles), :]).astype(jnp.bfloat16)
                 rows = slice(cycle * fields, (cycle + 1) * fields)
                 out[eo, rows, :n] = tile[:fields]
                 out[eo, rows, n:] = tile[fields:]
@@ -287,7 +289,7 @@
         all_blocks(p).wait_send()
 
 
-def wave_kernel(scale, sum_ref, held_ref, basis_ref, total_ref, out_hbm, energy_ref, out, out_sem):
+def wave_kernel(scale, sum_ref, held_ref, basis_ref, total_ref, out_hbm, energy_hbm, out, energy, out_sem, energy_sem):
     cycles, fields, _ = out.shape
     width = 256
     tiles = HALF // width
@@ -295,6 +297,9 @@
     def out_copy(tile, side):
         columns = pl.ds(pl.multiple_of(side * HALF + tile * width, width), width)
         return pltpu.make_async_copy(out.at[:, :, columns], out_hbm.at[:, :, columns], out_sem.at[tile, side])
+
+    energy[...] = (total_ref[:, :fields] + total_ref[:, fields:]) * scale
+    energy_copy = pltpu.make_async_copy(energy, energy_hbm, energy_sem)
 
     @pl.loop(0, tiles, unroll=8)
     def _(tile):
@@ -307,12 +312,14 @@
         for side in range(2):
             out_copy(tile, side).start()
 
-    energy_ref[...] = (total_ref[:, :fields] + total_ref[:, fields:]) * scale
+    energy_copy.start()
 
     @pl.loop(0, tiles)
     def _(tile):
         for side in range(2):
             out_copy(tile, side).wait()
+
+    energy_copy.wait()
 
 
 def shards(load_coef, legendre, slab_orders, cycle_rows):
@@ -352,7 +359,7 @@
             pltpu.VMEM((2 * pairs * streams, lat_count), jnp.bfloat16),
             pltpu.VMEM((pairs, n * per_peer, streams), jnp.bfloat16),
             pltpu.VMEM((pairs, n * per_peer, streams), jnp.bfloat16),
-            pltpu.VMEM((n * per_peer, streams), jnp.float32),
+            pltpu.VMEM((2, n * cycles, streams), jnp.float32),
             pltpu.VMEM((2, 1, streams), jnp.float32),
             pltpu.VMEM((COLUMN, 1, streams), jnp.float32),
             pltpu.VMEM((SPOTS, 1, streams), jnp.float32),
@@ -378,10 +385,12 @@
             jax.ShapeDtypeStruct((1, fields), jnp.float32),
         ],
         in_specs=[vmem] * 4,
-        out_specs=[anywhere, vmem],
+        out_specs=[anywhere, anywhere],
         scratch_shapes=[
             pltpu.VMEM((cycles, fields, NLON), jnp.bfloat16),
+            pltpu.VMEM((1, fields), jnp.float32),
             dma((HALF // 256, 2)),
+            dma,
         ],
         compiler_params=pltpu.CompilerParams(vmem_limit_bytes=24 * 2**20),
         name="wave",

time: 40.8 us -> 40.3 us (0.988)
  Pallas kernels: 40 us -> 39.5 us
    pallas_call x1, Pallas kernels: 2.96 us -> 2.47 us  [shards(): pl.pallas_call(functools.partial(wave_kernel, 1.0 / lat_count), out_shape...]
where the time goes in v5:
time: 40.3 us; the launch traced here: 40.2 us
  Pallas kernels  39.5 us (98%)
  between operations  0.64 us (2%)
    pallas_call x1, Pallas kernels, shards(): pl.pallas_call(exchange_kernel, out_shape=[jax.ShapeDtypeStruct((2, cycle...  37.1 us
    pallas_call x1, Pallas kernels, shards(): pl.pallas_call(functools.partial(wave_kernel, 1.0 / lat_count), out_shape...  2.47 us

profile of v5, /device:TPU:1, one launch (start us, length us, event | category | flops | bytes accessed | tf_op | source)
XLA Modules:
  0.0 40.2 jit_solution(5961725837891409951)
XLA Ops:
  0.6 37.1 %exchange.1 = (f32[2,512,2048]{2,1,0:T(8,128)S(1)}, bf16[2,512,256]{2,1,0:T(8,128)(2,1)S(1)}, bf16[2,256,2048]{2,1,0:T(8,128)(2,1)S(1)}, f32[1,128]{1,0:T(1,128)S(1)}) custom-call(bf16[2049,2,1024]{2,1,0:T(2,128)(2,1)} %bitcast.5, bf16[2049,2,128]{2,1,0:T(2,128)(2,1)} %bitcast.6, s32[8,128]{1,0:T(8,128)} %bitcast.7, s32[1,256]{1,0:T(1,128)} %bitcast.8), custom_call_target="tpu_custom_call" | custom-call | tf_op jit(solution)/shard_map/exchange/pallas_call | solution.py:339
  37.7 2.5 %wave.1 = (bf16[8,64,4096]{2,1,0:T(8,128)(2,1)}, f32[1,64]{1,0:T(1,128)}) custom-call(f32[2,512,2048]{2,1,0:T(8,128)S(1)} %get-tuple-element.8.sum_ref, bf16[2,512,256]{2,1,0:T(8,128)(2,1)S(1)} %get-tuple-element.9.held_ref, bf16[2,256,2048]{2,1,0:T(8,128)(2,1)S(1)} %get-tuple-element.10.basis_ref, f32[1,128]{1,0:T(1,128)S(1)} %get-tuple-element.11.total_ref), custom_call_target="tpu_custom_call" | custom-call | tf_op jit(solution)/shard_map/wave/pallas_call | solution.py:381

commit v6 on v5

--- a/solution.py
+++ b/solution.py
@@ -18,6 +18,7 @@
 PER_PLANE = SPOTS * CORES
 COLUMN = PLANES * CORES
 HOPS = (2, 1, 3, 0)
+FINAL_HOPS = ((2, 1, 0, 3), (2, 0, 3, 1), (2, 3, 0, 1), (1, 2, 0, 3))
 
 
 def even_order(low, degree):
@@ -152,14 +153,17 @@
 
     def send_plane(p, hop):
         target = lax.rem(plane + hop, PLANES)
-
-        @pl.loop(1 if hop == 0 else 0, PER_PLANE)
-        def _(i):
+        first = (1 if hop == 0 else 0) if isinstance(hop, int) else jnp.where(hop == 0, 1, 0)
+
+        def send_one(i, carry):
             peer = target * PER_PLANE + lax.rem(spot + i // CORES, SPOTS) * CORES + lax.rem(core + i, CORES)
             pltpu.make_async_remote_copy(
                 src_ref=send.at[p, block_rows(peer), :], dst_ref=recv.at[p, block_rows(me), :],
                 send_sem=send_sem.at[p], recv_sem=recv_sem.at[p],
                 device_id={"blk": peer}, device_id_type=MESH).start()
+            return carry
+
+        lax.fori_loop(first, PER_PLANE, send_one, 0)
 
     def all_blocks(p):
         whole = pl.ds(0, (n - 1) * per_peer)
@@ -215,8 +219,8 @@
     def _(j):
         far_copy(j).start()
 
-    for hop in HOPS:
-        send_plane(1, hop)
+    for step in range(PLANES):
+        send_plane(1, sum(jnp.where(plane == z, FINAL_HOPS[z][step], 0) for z in range(PLANES)))
 
     scale = 2.0 * math.pi / NLON
     source = lax.broadcasted_iota(jnp.int32, (n, n * pairs), 0)

time: 40.3 us -> 40.3 us (level)
  no operation moved by 1% of the time
where the time goes in v6:
time: 40.3 us; the launch traced here: 40.2 us
  Pallas kernels  39.5 us (98%)
  between operations  0.64 us (2%)
    pallas_call x1, Pallas kernels, shards(): pl.pallas_call(exchange_kernel, out_shape=[jax.ShapeDtypeStruct((2, cycle...  37.1 us
    pallas_call x1, Pallas kernels, shards(): pl.pallas_call(functools.partial(wave_kernel, 1.0 / lat_count), out_shape...  2.46 us

profile of v6, /device:TPU:1, one launch (start us, length us, event | category | flops | bytes accessed | tf_op | source)
XLA Modules:
  0.0 40.2 jit_solution(6907401680556119553)
XLA Ops:
  0.6 37.1 %exchange.1 = (f32[2,512,2048]{2,1,0:T(8,128)S(1)}, bf16[2,512,256]{2,1,0:T(8,128)(2,1)S(1)}, bf16[2,256,2048]{2,1,0:T(8,128)(2,1)S(1)}, f32[1,128]{1,0:T(1,128)S(1)}) custom-call(bf16[2049,2,1024]{2,1,0:T(2,128)(2,1)} %bitcast.5, bf16[2049,2,128]{2,1,0:T(2,128)(2,1)} %bitcast.6, s32[8,128]{1,0:T(8,128)} %bitcast.7, s32[1,256]{1,0:T(1,128)} %bitcast.8), custom_call_target="tpu_custom_call" | custom-call | tf_op jit(solution)/shard_map/exchange/pallas_call | solution.py:343
  37.7 2.5 %wave.1 = (bf16[8,64,4096]{2,1,0:T(8,128)(2,1)}, f32[1,64]{1,0:T(1,128)}) custom-call(f32[2,512,2048]{2,1,0:T(8,128)S(1)} %get-tuple-element.8.sum_ref, bf16[2,512,256]{2,1,0:T(8,128)(2,1)S(1)} %get-tuple-element.9.held_ref, bf16[2,256,2048]{2,1,0:T(8,128)(2,1)S(1)} %get-tuple-element.10.basis_ref, f32[1,128]{1,0:T(1,128)S(1)} %get-tuple-element.11.total_ref), custom_call_target="tpu_custom_call" | custom-call | tf_op jit(solution)/shard_map/wave/pallas_call | solution.py:385
